TPU v7x, 32 devices: a whole 2x2x4 slice. The times are simulated.
32 devices in a mesh: dp: 16 (over z, y, core), tensor: 2 (over x).
Axes of the slice: x: 2, y: 2, z: 4, core: 2. Of those that a mesh axis runs over, the one named last changes fastest.
Arguments:
- tokens: bfloat16 [12288, 2048], P('dp'), may hold values from -6 to 6
- cotangent: bfloat16 [12288, 2048], P('dp'), may hold values from -8 to 8
- w_query: float32 [2048, 2048], P('dp', 'tensor'), may hold values from -0.125 to 0.125
- w_keyval: float32 [2048, 256], P('dp'), may hold values from -0.125 to 0.125
- w_out: float32 [2048, 2048], P('dp', 'tensor'), may hold values from -1 to 1
- w_up: float32 [2048, 8192], P('dp', 'tensor'), may hold values from -0.125 to 0.125
- w_down: float32 [2048, 8192], P('dp', 'tensor'), may hold values from -0.0625 to 0.0625
- norm1_gain: float32 [2048], P('dp'), may hold values from 0.25 to 1.75
- norm1_bias: float32 [2048], P('dp'), may hold values from -3 to 3
- norm2_gain: float32 [2048], P('dp'), may hold values from 0.25 to 1.75
- norm2_bias: float32 [2048], P('dp'), may hold values from -3 to 3
- route: int32 [12288], replicated, may hold values from 0 to 12287, as said below
- lengths: int32 [16, 4], P('dp'), may hold values from 1 to 512, 768 in all within a row
Outputs:
- output: bfloat16 [12288, 2048], P('dp')
- grad_tokens: bfloat16 [12288, 2048], P('dp')
- grad_w_query: float32 [2048, 2048], P('dp', 'tensor')
- grad_w_keyval: float32 [2048, 256], P('dp')
- grad_w_out: float32 [2048, 2048], P('dp', 'tensor')
- grad_w_up: float32 [2048, 8192], P('dp', 'tensor')
- grad_w_down: float32 [2048, 8192], P('dp', 'tensor')
- grad_norm1_gain: float32 [2048], P('dp')
- grad_norm1_bias: float32 [2048], P('dp')
- grad_norm2_gain: float32 [2048], P('dp')
- grad_norm2_bias: float32 [2048], P('dp')
Inputs may be any that keep to these rules, and one draw needn't show every extreme that they name: route is a permutation of the 12288 places; places g * 768 to (g + 1) * 768 - 1 belong to index g of dp, and the 768 tokens of each index of dp name exactly 48 places of every index of dp. Row g lists the lengths of the 4 sequences at index g of dp in order; they sum to 768, and the longest of each row is exactly 512.
All inputs are finite; a program needn't handle non-finite values.
Results may differ from a plain program's by a relative error of at most 0.012.
The roundings to bfloat16 on the way count: a program that leaves them out, or rounds other values in their place, can miss the bound.
Values may be sent and summed in bfloat16 or wider, within the bound.
A program may use at most 320 MiB of HBM per device.

v0:
```python
import jax
import jax.numpy as jnp
from jax import lax
from jax.sharding import PartitionSpec as P

norm_eps = 1e-05


def layer_norm(values, gain_vector, shift_vector):
    row_mean = jnp.mean(values, axis=-1, keepdims=True)
    centered = values - row_mean
    spread = jnp.mean(centered * centered, axis=-1, keepdims=True)
    return centered * lax.rsqrt(spread + norm_eps) * gain_vector + shift_vector


def gelu_tanh(values):
    return jax.nn.gelu(values, approximate=True)


def visible_pairs(lengths_row, row_count):
    boundaries = jnp.cumsum(lengths_row)
    places = jnp.arange(row_count, dtype=jnp.int32)
    segment = jnp.sum((places[:, None] >= boundaries[None, :]).astype(jnp.int32), axis=1)
    return jnp.logical_and(segment[:, None] == segment[None, :], places[None, :] <= places[:, None])


def right_product(first_op, second_op):
    return lax.dot_general(
        first_op, second_op, (((1,), (1,)), ((), ())), preferred_element_type=jnp.float32
    )


def left_product(first_op, second_op):
    return lax.dot_general(
        first_op, second_op, (((0,), (0,)), ((), ())), preferred_element_type=jnp.float32
    )


def column_term(first_op, second_op):
    return left_product(first_op, second_op)


def masked_scores(query_heads, key_rows, visible, score_scale):
    scores = (
        jnp.einsum("qhd,kd->hqk", query_heads, key_rows, preferred_element_type=jnp.float32)
        * score_scale
    )
    return jnp.where(visible, scores, -1e30)


def per_device(
    tokens,
    cotangent,
    w_query,
    w_keyval,
    w_out,
    w_up,
    w_down,
    norm1_gain,
    norm1_bias,
    norm2_gain,
    norm2_bias,
    route,
    lengths,
):
    row_count = tokens.shape[0]
    head_dim = w_keyval.shape[1] // 2
    heads_here = w_query.shape[1] // head_dim
    score_scale = head_dim ** (-0.5)
    group_index = lax.axis_index("dp")
    own_route = lax.dynamic_slice_in_dim(route, group_index * row_count, row_count)
    send_order = jnp.argsort(own_route, stable=True)
    inverse = jnp.argsort(route, stable=True)
    sources = lax.dynamic_slice_in_dim(inverse, group_index * row_count, row_count) // row_count
    recv_order = jnp.argsort(sources, stable=True)
    placing = jnp.argsort(recv_order, stable=True)
    arrived = (
        lax.all_to_all(tokens[send_order], "dp", split_axis=0, concat_axis=0, tiled=True),
        lax.all_to_all(cotangent[send_order], "dp", split_axis=0, concat_axis=0, tiled=True),
    )
    tokens_here = arrived[0][placing]
    grad_here = arrived[1][placing]
    fetched = (
        lax.all_gather(w_query.astype(jnp.bfloat16), "dp", axis=0, tiled=True),
        lax.all_gather(w_keyval.astype(jnp.bfloat16), "dp", axis=0, tiled=True),
        lax.all_gather(w_out.astype(jnp.bfloat16), "dp", axis=0, tiled=True),
        lax.all_gather(w_up.astype(jnp.bfloat16), "dp", axis=0, tiled=True),
        lax.all_gather(w_down.astype(jnp.bfloat16), "dp", axis=0, tiled=True),
        lax.all_gather(norm1_gain.astype(jnp.bfloat16), "dp", axis=0, tiled=True),
        lax.all_gather(norm1_bias.astype(jnp.bfloat16), "dp", axis=0, tiled=True),
        lax.all_gather(norm2_gain.astype(jnp.bfloat16), "dp", axis=0, tiled=True),
        lax.all_gather(norm2_bias.astype(jnp.bfloat16), "dp", axis=0, tiled=True),
    )
    full_query, full_keyval, full_out, full_up, full_down = (
        fetched[0],
        fetched[1],
        fetched[2],
        fetched[3],
        fetched[4],
    )
    first_gain = fetched[5].astype(jnp.float32)
    first_shift = fetched[6].astype(jnp.float32)
    second_gain = fetched[7].astype(jnp.float32)
    second_shift = fetched[8].astype(jnp.float32)
    resid_in = tokens_here.astype(jnp.float32)
    normed_one = layer_norm(resid_in, first_gain, first_shift).astype(jnp.bfloat16)
    queries = jnp.dot(normed_one, full_query, preferred_element_type=jnp.float32).astype(
        jnp.bfloat16
    )
    keyval = jnp.dot(normed_one, full_keyval, preferred_element_type=jnp.float32).astype(
        jnp.bfloat16
    )
    query_heads = queries.reshape(row_count, heads_here, head_dim)
    key_rows = keyval[:, :head_dim]
    value_rows = keyval[:, head_dim:]
    visible = visible_pairs(lengths[0], row_count)[None]
    masked = masked_scores(query_heads, key_rows, visible, score_scale)
    row_max = jnp.max(masked, axis=2, keepdims=True)
    weights_exp = jnp.exp(masked - row_max)
    row_total = jnp.sum(weights_exp, axis=2, keepdims=True)
    probs_first = (weights_exp / row_total).astype(jnp.bfloat16)
    log_total = row_max + jnp.log(row_total)
    context = jnp.einsum("hqk,kd->qhd", probs_first, value_rows, preferred_element_type=jnp.float32)
    context = context.reshape(row_count, heads_here * head_dim).astype(jnp.bfloat16)
    attn_output = lax.psum(right_product(context, full_out), "tensor")
    resid_mid = resid_in + attn_output
    normed_two = layer_norm(resid_mid, second_gain, second_shift).astype(jnp.bfloat16)
    hidden_pre = jnp.dot(normed_two, full_up, preferred_element_type=jnp.float32)
    active = gelu_tanh(hidden_pre).astype(jnp.bfloat16)
    mlp_output = lax.psum(right_product(active, full_down).astype(jnp.bfloat16), "tensor").astype(
        jnp.float32
    )
    result = (resid_mid + mlp_output).astype(jnp.bfloat16)
    refetched = (
        lax.all_gather(w_query.astype(jnp.bfloat16), "dp", axis=0, tiled=True),
        lax.all_gather(w_keyval.astype(jnp.bfloat16), "dp", axis=0, tiled=True),
        lax.all_gather(w_out.astype(jnp.bfloat16), "dp", axis=0, tiled=True),
        lax.all_gather(w_up.astype(jnp.bfloat16), "dp", axis=0, tiled=True),
        lax.all_gather(w_down.astype(jnp.bfloat16), "dp", axis=0, tiled=True),
    )
    back_query, back_keyval, back_out, back_up, back_down = (
        refetched[0],
        refetched[1],
        refetched[2],
        refetched[3],
        refetched[4],
    )
    grad_out = grad_here.astype(jnp.float32)
    grad_active = jnp.dot(grad_here, back_down, preferred_element_type=jnp.float32)
    gelu_back = jax.vjp(gelu_tanh, hidden_pre)[1]
    grad_up = gelu_back(grad_active)[0].astype(jnp.bfloat16)
    grad_norm_two = lax.psum(right_product(grad_up, back_up), "tensor")
    norm_two_back = jax.vjp(layer_norm, resid_mid, second_gain, second_shift)[1]
    grad_mid_norm, grad_gain_two, grad_shift_two = norm_two_back(grad_norm_two)
    grad_mid = grad_out + grad_mid_norm
    grad_mid_low = grad_mid.astype(jnp.bfloat16)
    grad_context = jnp.dot(grad_mid_low, back_out, preferred_element_type=jnp.float32).astype(
        jnp.bfloat16
    )
    grad_ctx_heads = grad_context.reshape(row_count, heads_here, head_dim)
    masked_again = masked_scores(query_heads, key_rows, visible, score_scale)
    probs_again = jnp.exp(masked_again - log_total)
    probs_low = probs_again.astype(jnp.bfloat16)
    grad_probs = jnp.einsum(
        "qhd,kd->hqk", grad_ctx_heads, value_rows, preferred_element_type=jnp.float32
    )
    row_delta = jnp.sum(grad_probs * probs_again, axis=2, keepdims=True)
    grad_scores = (probs_again * (grad_probs - row_delta)).astype(jnp.bfloat16)
    grad_query = (
        jnp.einsum("hqk,kd->qhd", grad_scores, key_rows, preferred_element_type=jnp.float32)
        * score_scale
    )
    grad_query = grad_query.reshape(row_count, heads_here * head_dim).astype(jnp.bfloat16)
    grad_keys = (
        jnp.einsum("hqk,qhd->kd", grad_scores, query_heads, preferred_element_type=jnp.float32)
        * score_scale
    )
    grad_values = jnp.einsum(
        "hqk,qhd->kd", probs_low, grad_ctx_heads, preferred_element_type=jnp.float32
    )
    grad_keyval_part = jnp.concatenate([grad_keys, grad_values], axis=1)
    grad_norm_query, grad_keyval = lax.psum(
        (right_product(grad_query, back_query), grad_keyval_part), "tensor"
    )
    grad_keyval_low = grad_keyval.astype(jnp.bfloat16)
    grad_norm_one = grad_norm_query + right_product(grad_keyval_low, back_keyval)
    norm_one_back = jax.vjp(layer_norm, resid_in, first_gain, first_shift)[1]
    grad_in_norm, grad_gain_one, grad_shift_one = norm_one_back(grad_norm_one)
    grad_resid = (grad_mid + grad_in_norm).astype(jnp.bfloat16)
    edge_one = w_query.shape[1]
    edge_two = edge_one + w_keyval.shape[1]
    up_cols = w_up.shape[1]
    summed = lax.psum_scatter(
        jnp.concatenate(
            [
                column_term(normed_one, grad_query),
                column_term(normed_one, grad_keyval_low),
                column_term(grad_mid_low, context),
                column_term(normed_two, grad_up),
                column_term(grad_here, active),
            ],
            axis=1,
        ),
        "dp",
        scatter_dimension=0,
        tiled=True,
    )
    edge_three = edge_two + w_out.shape[1]
    edge_four = edge_three + up_cols
    grad_wq = summed[:, :edge_one]
    grad_wkv = summed[:, edge_one:edge_two]
    grad_wo = summed[:, edge_two:edge_three]
    grad_wup = summed[:, edge_three:edge_four]
    grad_wdown = summed[:, edge_four:]
    norm_parts = (
        lax.psum_scatter(grad_gain_one, "dp", scatter_dimension=0, tiled=True),
        lax.psum_scatter(grad_shift_one, "dp", scatter_dimension=0, tiled=True),
        lax.psum_scatter(grad_gain_two, "dp", scatter_dimension=0, tiled=True),
        lax.psum_scatter(grad_shift_two, "dp", scatter_dimension=0, tiled=True),
    )
    returned = (
        lax.all_to_all(result[recv_order], "dp", split_axis=0, concat_axis=0, tiled=True),
        lax.all_to_all(grad_resid[recv_order], "dp", split_axis=0, concat_axis=0, tiled=True),
    )
    restore = jnp.argsort(send_order, stable=True)
    output = returned[0][restore]
    grad_tokens = returned[1][restore]
    return (
        output,
        grad_tokens,
        grad_wq,
        grad_wkv,
        grad_wo,
        grad_wup,
        grad_wdown,
        norm_parts[0],
        norm_parts[1],
        norm_parts[2],
        norm_parts[3],
    )


def solution(mesh):
    placed = (
        P("dp", None),
        P("dp", None),
        P("dp", "tensor"),
        P("dp", None),
        P("dp", "tensor"),
        P("dp", "tensor"),
        P("dp", "tensor"),
        P("dp"),
        P("dp"),
        P("dp"),
        P("dp"),
        P(),
        P("dp", None),
    )
    return jax.shard_map(
        per_device,
        mesh=mesh,
        in_specs=placed,
        out_specs=(
            P("dp", None),
            P("dp", None),
            P("dp", "tensor"),
            P("dp", None),
            P("dp", "tensor"),
            P("dp", "tensor"),
            P("dp", "tensor"),
            P("dp"),
            P("dp"),
            P("dp"),
            P("dp"),
        ),
        check_vma=False,
    )
```

profile of v0, /device:TPU:0, one launch (start us, length us, event | category | flops | bytes accessed | tf_op | source)
XLA Modules:
  0.0 1982.8 jit_solution(17851792786017311539)
XLA Ops:
  29.9 69.7 %all-gather.1 = bf16[16,1,128]{2,1,0:T(2,128)(2,1)S(1)} all-gather(bf16[1,1,128]{2,1,0:T(2,128)(2,1)S(1)} %convert_bitcast_fusion.2), channel_id=1, replica_groups=mesh['dp'=16,'tensor'=2] {'dp'}, dimensions={0}, use_global_device_ids=true | all-gather | bytes 4352 | tf_op jit(solution)/shard_map/all_gather | solution.py:90
  99.6 48.6 %all-gather = bf16[16,1,128]{2,1,0:T(2,128)(2,1)S(1)} all-gather(bf16[1,1,128]{2,1,0:T(2,128)(2,1)S(1)} %convert_bitcast_fusion.3), channel_id=1, replica_groups=mesh['dp'=16,'tensor'=2] {'dp'}, dimensions={0}, use_global_device_ids=true | all-gather | bytes 4352 | tf_op jit(solution)/shard_map/all_gather | solution.py:89
  192.4 9.4 fusion.47
  242.1 67.0 %all-gather.3 = bf16[16,1,128]{2,1,0:T(2,128)(2,1)S(1)} all-gather(bf16[1,1,128]{2,1,0:T(2,128)(2,1)S(1)} %convert_bitcast_fusion), channel_id=1, replica_groups=mesh['dp'=16,'tensor'=2] {'dp'}, dimensions={0}, use_global_device_ids=true | all-gather | bytes 4352 | tf_op jit(solution)/shard_map/all_gather | solution.py:92
  309.2 32.8 %all-gather.2 = bf16[16,1,128]{2,1,0:T(2,128)(2,1)S(1)} all-gather(bf16[1,1,128]{2,1,0:T(2,128)(2,1)S(1)} %convert_bitcast_fusion.1), channel_id=1, replica_groups=mesh['dp'=16,'tensor'=2] {'dp'}, dimensions={0}, use_global_device_ids=true | all-gather | bytes 4352 | tf_op jit(solution)/shard_map/all_gather | solution.py:91
  346.7 31.9 %all-reduce.11.cloned.1.call-done = f32[768,2048]{1,0:T(8,128)} async-done(((f32[768,2048]{1,0:T(8,128)}), f32[768,2048]{1,0:T(8,128)}) %all-reduce.11.cloned.1.call-update) | async-done | bytes 6291472 | tf_op jit(solution)/shard_map/psum | solution.py:125
  386.9 120.7 %all-gather.18.cloned.1.call-done = bf16[2048,4096]{1,0:T(8,128)(2,1)} async-done(((bf16[128,4096]{1,0:T(8,128)(2,1)}), bf16[2048,4096]{1,0:T(8,128)(2,1)}) %all-gather.18.cloned.1.call-update) | async-done | bytes 16777232 | tf_op jit(solution)/shard_map/all_gather | solution.py:88
  507.6 19.3 fusion.49
  526.9 107.9 %all-gather.16.cloned.1.call-done = bf16[2048,4096]{1,0:T(8,128)(2,1)} async-done(((bf16[128,4096]{1,0:T(8,128)(2,1)}), bf16[2048,4096]{1,0:T(8,128)(2,1)}) %all-gather.16.cloned.1.call-update) | async-done | bytes 16777232 | tf_op jit(solution)/shard_map/all_gather | solution.py:87
  634.8 30.8 %fusion.11 = (bf16[768,4096]{1,0:T(8,128)(2,1)}, f32[768,4096]{1,0:T(8,128)}) fusion(f32[768,4096]{1,0:T(8,128)} %fusion.49, bf16[2048,4096]{1,0:T(8,128)(2,1)} %all-gather.16.cloned.1.call-done, f32[768,2048]{1,0:T(8,128)} %copy-done.5, f32[2048]{0:T(1024)S(1)} %bitcast.116, f32[2048]{0:T(1024)S(1)} %bitcast.111, f32[768]{0:T(1024)S(1)} %fusion.39, ...), kind=kOutput, calls=%fused_computation.29 | convolution fusion | flops 12955680768 | bytes 54548480 | tf_op jit(solution)/shard_map/dot_general | solution.py:128
  665.7 20.5 %fusion.50 = f32[768,2048]{1,0:T(8,128)} fusion(bf16[768,4096]{1,0:T(8,128)(2,1)} %get-tuple-element.43, bf16[2048,4096]{1,0:T(8,128)(2,1)} %all-gather.16.cloned.1.call-done), kind=kOutput, calls=%fused_computation.118 | convolution fusion | flops 12884901888 | bytes 29360128 | tf_op jit(solution)/shard_map/dot_general | solution.py:28
  686.3 31.9 %convolution_convert_fusion = bf16[768,2048]{1,0:T(8,128)(2,1)} fusion(bf16[2048,4096]{1,0:T(8,128)(2,1)} %all-gather.18.cloned.1.call-done, f32[768,4096]{1,0:T(8,128)} %get-tuple-element.44), kind=kOutput, calls=%fused_computation.61 | convolution fusion | flops 12914786304 | bytes 32505856 | tf_op jit(solution)/shard_map/dot_general | solution.py:28
  718.3 119.5 %all-reduce.15.cloned.1.call-done = f32[768,2048]{1,0:T(8,128)} async-done(((f32[768,2048]{1,0:T(8,128)}), f32[768,2048]{1,0:T(8,128)}) %all-reduce.15.cloned.1.call-update) | async-done | bytes 6291472 | tf_op jit(solution)/shard_map/psum | solution.py:152
  844.6 81.4 %all-reduce.13.cloned.1.call-done = bf16[768,2048]{1,0:T(8,128)(2,1)} async-done(((bf16[768,2048]{1,0:T(8,128)(2,1)}), bf16[768,2048]{1,0:T(8,128)(2,1)}) %all-reduce.13.cloned.1.call-update) | async-done | bytes 3145744 | tf_op jit(solution)/shard_map/psum | solution.py:130
  953.8 12.1 fusion
  965.9 12.9 fusion.2
  985.5 22.9 %all-reduce.18 = bf16[768,256]{0,1:T(8,128)(2,1)S(1)} all-reduce(f32[768,256]{0,1:T(8,128)} %pad_maximum_fusion), channel_id=1, replica_groups=mesh['dp'=16,'tensor'=2] {'tensor'}, use_global_device_ids=true, to_apply=%region_20.21 | all-reduce | flops 196608 | bytes 1179648 | tf_op jit(solution)/shard_map/psum | solution.py:182
  1033.7 23.6 %convolution_dynamic-update-slice_fusion.1 = f32[2048,10496]{1,0:T(8,128)} fusion(f32[2048,10496]{1,0:T(8,128)} %convolution_dynamic-update-slice_fusion.2, bf16[768,4096]{1,0:T(8,128)(2,1)} %get-tuple-element.43, f32[768,2048]{1,0:T(8,128)} %copy-done.5, f32[2048]{0:T(1024)S(1)} %bitcast.117, f32[2048]{0:T(1024)S(1)} %bitcast.114, f32[768]{0:T(1024)S(1)} %fusion.39, ...), kind=kOutput, calls=%fused_computation.9 | convolution fusion | flops 12892766208 | bytes 46159872 | tf_op jit(solution)/shard_map/dot_general | solution.py:34
  1057.3 25.4 %convolution_dynamic-update-slice_fusion = f32[2048,10496]{1,0:T(8,128)} fusion(f32[2048,10496]{1,0:T(8,128)} %convolution_dynamic-update-slice_fusion.1, bf16[768,2048]{1,0:T(8,128)(2,1)} %gather_fusion.5, f32[768,4096]{1,0:T(8,128)} %get-tuple-element.44), kind=kOutput, calls=%fused_computation.8 | convolution fusion | flops 12913213440 | bytes 49283072 | tf_op jit(solution)/shard_map/dot_general | solution.py:34
  1094.2 83.2 %all-reduce.17.cloned.1.call-done = f32[768,2048]{1,0:T(8,128)} async-done(((f32[768,2048]{1,0:T(8,128)}), f32[768,2048]{1,0:T(8,128)}) %all-reduce.17.cloned.1.call-update) | async-done | bytes 6291472 | tf_op jit(solution)/shard_map/psum | solution.py:182
  1192.8 10.1 gather_fusion.6
  1219.1 100.9 %all-reduce.4 = (f32[2048]{0:T(1024)S(1)}, f32[2048]{0:T(1024)S(1)}, f32[2048]{0:T(1024)S(1)}, f32[2048]{0:T(1024)S(1)}) all-reduce(f32[2048]{0:T(1024)S(1)} %get-tuple-element.23, f32[2048]{0:T(1024)S(1)} %copy-done.36, f32[2048]{0:T(1024)S(1)} %copy-done.37, f32[2048]{0:T(1024)S(1)} %copy-done.38), channel_id=3, replica_groups=mesh['dp'=16,'tensor'=2] {'dp'}, use_global_device_ids=true, to_apply=%region_25.26.clone | all-reduce | flops 8192 | bytes 65536
  1322.3 9.6 gather_fusion.7
  1331.9 635.1 %reduce-scatter.2.cloned.1.call-done = f32[128,10496]{1,0:T(8,128)} async-done(((f32[2048,10496]{1,0:T(8,128)}), f32[128,10496]{1,0:T(8,128)}) %reduce-scatter.2.cloned.1.call-update) | async-done | bytes 5373968 | tf_op jit(solution)/shard_map/reduce_scatter | solution.py:193
  (227 shorter events, 239.7 us)
Async XLA Ops:
  7.2 173.3 %all-gather.10.cloned.1.call-start = ((), (), s32[]{:S(2)}) async-start(), calls=%async_computation.5 | async-start | bytes 1114112 | tf_op jit(solution)/shard_map/all_gather | solution.py:85
  9.0 174.9 %all-gather.12.cloned.1.call-start = ((), (), s32[]{:S(2)}) async-start(), calls=%async_computation.6 | async-start | bytes 4456448 | tf_op jit(solution)/shard_map/all_gather | solution.py:84
  20.2 128.1 %copy-start.29 = (s32[12288]{0:T(1024)S(1)}, s32[12288]{0:T(1024)}, u32[]{:S(2)}) copy-start(s32[12288]{0:T(1024)} %param.24) | copy-start | bytes 147460
  20.3 146.4 %all-to-all-start = ((bf16[16,48,2048]{2,1,0:T(8,128)(2,1)}), bf16[16,48,2048]{2,1,0:T(8,128)(2,1)S(1)}, u32[]{:S(2)}, u32[]{:S(2)}) async-start(bf16[16,48,2048]{2,1,0:T(8,128)(2,1)} %bitcast.99), calls=%async_computation | async-start | bytes 6291456 | tf_op jit(solution)/shard_map/all_to_all | solution.py:78
  27.8 191.8 %all-gather.14.cloned.1.call-start = ((), (), s32[]{:S(2)}) async-start(), calls=%async_computation.7 | async-start | bytes 4456448 | tf_op jit(solution)/shard_map/all_gather | solution.py:86
  29.7 348.9 %all-reduce.11.cloned.1.call-start = ((), (), s32[]{:S(2)}) async-start(), calls=%async_computation.8 | async-start | bytes 12582912 | tf_op jit(solution)/shard_map/psum | solution.py:125
  227.9 279.7 %all-gather.18.cloned.1.call-start = ((), (), s32[]{:S(2)}) async-start(), calls=%async_computation.10 | async-start | bytes 17825792 | tf_op jit(solution)/shard_map/all_gather | solution.py:88
  230.8 404.0 %all-gather.16.cloned.1.call-start = ((), (), s32[]{:S(2)}) async-start(), calls=%async_computation.9 | async-start | bytes 17825792 | tf_op jit(solution)/shard_map/all_gather | solution.py:87
  238.2 71.0 %copy-start.51 = (f32[128]{0:T(128)S(1)}, f32[128]{0:T(128)}, u32[]{:S(2)}) copy-start(f32[128]{0:T(128)} %param.22) | copy-start | bytes 1540
  238.2 103.8 %all-to-all-start.2 = ((bf16[16,48,2048]{2,1,0:T(8,128)(2,1)}), bf16[16,48,2048]{2,1,0:T(8,128)(2,1)S(1)}, u32[]{:S(2)}, u32[]{:S(2)}) async-start(bf16[16,48,2048]{2,1,0:T(8,128)(2,1)} %bitcast.102), calls=%async_computation.2 | async-start | bytes 6291456 | tf_op jit(solution)/shard_map/all_to_all | solution.py:79
  242.1 595.7 %all-reduce.15.cloned.1.call-start = ((), (), s32[]{:S(2)}) async-start(), calls=%async_computation.12 | async-start | bytes 12582912 | tf_op jit(solution)/shard_map/psum | solution.py:152
  309.1 325.7 %copy-start.43 = (f32[16,1,128]{2,1,0:T(1,128)}, f32[16,1,128]{2,1,0:T(1,128)S(1)}, u32[]{:S(2)}) copy-start(f32[16,1,128]{2,1,0:T(1,128)S(1)} %convert_element_type.160) | copy-start | bytes 24580
  382.9 124.7 %copy-start.7 = (bf16[768,2048]{1,0:T(8,128)(2,1)S(1)}, bf16[768,2048]{1,0:T(8,128)(2,1)}, u32[]{:S(2)}) copy-start(bf16[768,2048]{1,0:T(8,128)(2,1)} %gather_fusion.5) | copy-start | bytes 9437188
  686.2 239.7 %all-reduce.13.cloned.1.call-start = ((), (), s32[]{:S(2)}) async-start(), calls=%async_computation.11 | async-start | bytes 6291456 | tf_op jit(solution)/shard_map/psum | solution.py:130
  686.3 32.0 %copy-start.20 = (f32[8,768]{1,0:T(8,128)S(1)}, f32[8,768]{1,0:T(8,128)}, u32[]{:S(2)}) copy-start(f32[8,768]{1,0:T(8,128)} %copy-done.19) | copy-start | bytes 73732
  686.3 32.0 %copy-start.26 = (f32[8,768]{1,0:T(8,128)S(1)}, f32[8,768]{1,0:T(8,128)}, u32[]{:S(2)}) copy-start(f32[8,768]{1,0:T(8,128)} %copy-done.25) | copy-start | bytes 73732
  718.2 459.1 %all-reduce.17.cloned.1.call-start = ((), (), s32[]{:S(2)}) async-start(), calls=%async_computation.13 | async-start | bytes 12582912 | tf_op jit(solution)/shard_map/psum | solution.py:182
  1023.1 943.8 %reduce-scatter.2.cloned.1.call-start = ((), (), s32[]{:S(2)}) async-start(), calls=%async_computation.14 | async-start | bytes 91357184 | tf_op jit(solution)/shard_map/reduce_scatter | solution.py:193
  1088.3 89.1 %copy-start.22 = (f32[16,1,128]{2,1,0:T(1,128)S(1)}, f32[16,1,128]{2,1,0:T(1,128)}, u32[]{:S(2)}) copy-start(f32[16,1,128]{2,1,0:T(1,128)} %copy-done.21) | copy-start | bytes 24580
  1088.3 89.1 %copy-start.24 = (f32[768]{0:T(1024)S(1)}, f32[768]{0:T(1024)}, u32[]{:S(2)}) copy-start(f32[768]{0:T(1024)} %copy-done.23) | copy-start | bytes 9220
  1088.3 114.7 %all-to-all-start.1 = ((bf16[16,48,2048]{2,1,0:T(8,128)(2,1)}), bf16[16,48,2048]{2,1,0:T(8,128)(2,1)S(1)}, u32[]{:S(2)}, u32[]{:S(2)}) async-start(bf16[16,48,2048]{2,1,0:T(8,128)(2,1)} %bitcast.101), calls=%async_computation.1 | async-start | bytes 6291456 | tf_op jit(solution)/shard_map/all_to_all | solution.py:222
  1094.1 89.3 %copy-start.28 = (f32[768]{0:T(1024)S(1)}, f32[768]{0:T(1024)}, u32[]{:S(2)}) copy-start(f32[768]{0:T(1024)} %copy-done.27) | copy-start | bytes 9220
  1203.0 119.4 %all-to-all-start.3 = ((bf16[16,48,2048]{2,1,0:T(8,128)(2,1)}), bf16[16,48,2048]{2,1,0:T(8,128)(2,1)}, u32[]{:S(2)}, u32[]{:S(2)}) async-start(bf16[16,48,2048]{2,1,0:T(8,128)(2,1)} %bitcast.100), calls=%async_computation.3 | async-start | bytes 6291456 | tf_op jit(solution)/shard_map/all_to_all | solution.py:223
  1322.3 653.2 %copy-start.1 = (bf16[768,2048]{1,0:T(8,128)(2,1)S(1)}, bf16[768,2048]{1,0:T(8,128)(2,1)}, u32[]{:S(2)}) copy-start(bf16[768,2048]{1,0:T(8,128)(2,1)} %param.13) | copy-start | bytes 9437188
  (45 other events, 310.0 us)
Sparse Core Ops, SparseCore 0:
  10.7 62.2 all-gather.9
  75.7 56.6 all-gather.11
  134.6 50.0 all-gather.13
  228.0 150.5 all-reduce.10
  381.1 126.4 all-gather.17
  510.2 124.5 all-gather.15
  686.3 151.4 all-reduce.14
  840.1 85.8 all-reduce.12
  1023.3 154.0 all-reduce.16
  1181.4 785.5 reduce-scatter.1
where the time goes:
time: 1990 us; the launch traced here: 1980 us
  waiting for transfers between devices  1180 us (59%)
  blocking collectives  342 us (17%)
  matrix products  250 us (13%)
  other arithmetic  98.3 us (5%)
  local copies, waits for them, and re-layouts  72.6 us (4%)
  starting transfers between devices  23.9 us (1%)
    reduce_scatter x1, waiting for transfers between devices, per_device(): lax.psum_scatter(jnp.concatenate([column_term(normed_one, grad_query), co...  635 us
    all_gather x1, waiting for transfers between devices, per_device(): lax.all_gather(w_down.astype(jnp.bfloat16), 'dp', axis=0, tiled=True)  121 us
    psum x1, waiting for transfers between devices, per_device(): grad_norm_two = lax.psum(right_product(grad_up, back_up), 'tensor')  120 us
    all_gather x1, waiting for transfers between devices, per_device(): lax.all_gather(w_up.astype(jnp.bfloat16), 'dp', axis=0, tiled=True)  108 us
    unnamed x1, blocking collectives  101 us
    psum x1, waiting for transfers between devices, per_device(): lax.psum((right_product(grad_query, back_query), grad_keyval_part), 'tens...  83.2 us
    psum x1, waiting for transfers between devices, per_device(): lax.psum(right_product(active, full_down).astype(jnp.bfloat16), 'tensor')  81.4 us
    dot_general x5, matrix products, right_product(): lax.dot_general(first_op, second_op, (((1,), (1,)), ((), ())), preferred_...  72.1 us
  transfers between devices with their start and end apart: 14, of which 7 were waited for; matrix products, arithmetic and copies ran while one was open for 14% of the time, Pallas kernels for 0%

commit v1 on v0

--- a/solution.py
+++ b/solution.py
@@ -127,9 +127,9 @@
     normed_two = layer_norm(resid_mid, second_gain, second_shift).astype(jnp.bfloat16)
     hidden_pre = jnp.dot(normed_two, full_up, preferred_element_type=jnp.float32)
     active = gelu_tanh(hidden_pre).astype(jnp.bfloat16)
-    mlp_output = lax.psum(right_product(active, full_down).astype(jnp.bfloat16), "tensor").astype(
-        jnp.float32
-    )
+    mlp_output = jnp.sum(
+        jax.lax.all_gather(right_product(active, full_down).astype(jnp.bfloat16), "tensor"), axis=0
+    ).astype(jnp.float32)
     result = (resid_mid + mlp_output).astype(jnp.bfloat16)
     refetched = (
         lax.all_gather(w_query.astype(jnp.bfloat16), "dp", axis=0, tiled=True),

time: 1990 us -> 1990 us (level)
    psum x1 -> x0, waiting for transfers between devices: 81.4 us -> none  [per_device(): lax.psum(right_product(active, full_down).astype(jnp.bfloat16), 'tensor')]
    all_gather x0 -> x1, waiting for transfers between devices: none -> 75.4 us  [per_device(): jax.lax.all_gather(right_product(active, full_down).astype(jnp.bfloat16),...]
where the time goes in v1:
time: 1990 us; the launch traced here: 1980 us
  waiting for transfers between devices  1170 us (59%)
  blocking collectives  342 us (17%)
  matrix products  251 us (13%)
  other arithmetic  105 us (5%)
  local copies, waits for them, and re-layouts  72.5 us (4%)
  starting transfers between devices  23.8 us (1%)
    reduce_scatter x1, waiting for transfers between devices, per_device(): lax.psum_scatter(jnp.concatenate([column_term(normed_one, grad_query), co...  635 us
    all_gather x1, waiting for transfers between devices, per_device(): lax.all_gather(w_down.astype(jnp.bfloat16), 'dp', axis=0, tiled=True)  121 us
    psum x1, waiting for transfers between devices, per_device(): grad_norm_two = lax.psum(right_product(grad_up, back_up), 'tensor')  120 us
    all_gather x1, waiting for transfers between devices, per_device(): lax.all_gather(w_up.astype(jnp.bfloat16), 'dp', axis=0, tiled=True)  108 us
    unnamed x1, blocking collectives  101 us
    psum x1, waiting for transfers between devices, per_device(): lax.psum((right_product(grad_query, back_query), grad_keyval_part), 'tens...  83.1 us
    all_gather x1, waiting for transfers between devices, per_device(): jax.lax.all_gather(right_product(active, full_down).astype(jnp.bfloat16),...  75.4 us
    dot_general x5, matrix products, right_product(): lax.dot_general(first_op, second_op, (((1,), (1,)), ((), ())), preferred_...  72.4 us
  transfers between devices with their start and end apart: 14, of which 7 were waited for; matrix products, arithmetic and copies ran while one was open for 14% of the time, Pallas kernels for 0%

profile of v1, /device:TPU:0, one launch (start us, length us, event | category | flops | bytes accessed | tf_op | source)
XLA Modules:
  0.0 1983.5 jit_solution(15407352050042404907)
XLA Ops:
  30.0 69.7 %all-gather.2 = bf16[16,1,128]{2,1,0:T(2,128)(2,1)S(1)} all-gather(bf16[1,1,128]{2,1,0:T(2,128)(2,1)S(1)} %convert_bitcast_fusion.2), channel_id=1, replica_groups=mesh['dp'=16,'tensor'=2] {'dp'}, dimensions={0}, use_global_device_ids=true | all-gather | bytes 4352 | tf_op jit(solution)/shard_map/all_gather | solution.py:90
  99.6 48.6 %all-gather.1 = bf16[16,1,128]{2,1,0:T(2,128)(2,1)S(1)} all-gather(bf16[1,1,128]{2,1,0:T(2,128)(2,1)S(1)} %convert_bitcast_fusion.3), channel_id=1, replica_groups=mesh['dp'=16,'tensor'=2] {'dp'}, dimensions={0}, use_global_device_ids=true | all-gather | bytes 4352 | tf_op jit(solution)/shard_map/all_gather | solution.py:89
  192.7 9.4 fusion.47
  242.4 67.0 %all-gather.4 = bf16[16,1,128]{2,1,0:T(2,128)(2,1)S(1)} all-gather(bf16[1,1,128]{2,1,0:T(2,128)(2,1)S(1)} %convert_bitcast_fusion), channel_id=1, replica_groups=mesh['dp'=16,'tensor'=2] {'dp'}, dimensions={0}, use_global_device_ids=true | all-gather | bytes 4352 | tf_op jit(solution)/shard_map/all_gather | solution.py:92
  309.4 32.8 %all-gather.3 = bf16[16,1,128]{2,1,0:T(2,128)(2,1)S(1)} all-gather(bf16[1,1,128]{2,1,0:T(2,128)(2,1)S(1)} %convert_bitcast_fusion.1), channel_id=1, replica_groups=mesh['dp'=16,'tensor'=2] {'dp'}, dimensions={0}, use_global_device_ids=true | all-gather | bytes 4352 | tf_op jit(solution)/shard_map/all_gather | solution.py:91
  346.7 32.1 %all-reduce.10.cloned.1.call-done = f32[768,2048]{1,0:T(8,128)} async-done(((f32[768,2048]{1,0:T(8,128)}), f32[768,2048]{1,0:T(8,128)}) %all-reduce.10.cloned.1.call-update) | async-done | bytes 6291472 | tf_op jit(solution)/shard_map/psum | solution.py:125
  387.1 120.7 %all-gather.20.cloned.1.call-done = bf16[2048,4096]{1,0:T(8,128)(2,1)} async-done(((bf16[128,4096]{1,0:T(8,128)(2,1)}), bf16[2048,4096]{1,0:T(8,128)(2,1)}) %all-gather.20.cloned.1.call-update) | async-done | bytes 16777232 | tf_op jit(solution)/shard_map/all_gather | solution.py:88
  507.8 19.3 fusion.49
  527.2 107.9 %all-gather.18.cloned.1.call-done = bf16[2048,4096]{1,0:T(8,128)(2,1)} async-done(((bf16[128,4096]{1,0:T(8,128)(2,1)}), bf16[2048,4096]{1,0:T(8,128)(2,1)}) %all-gather.18.cloned.1.call-update) | async-done | bytes 16777232 | tf_op jit(solution)/shard_map/all_gather | solution.py:87
  635.0 30.9 %fusion.11 = (bf16[768,4096]{1,0:T(8,128)(2,1)}, f32[768,4096]{1,0:T(8,128)}) fusion(f32[768,4096]{1,0:T(8,128)} %fusion.49, bf16[2048,4096]{1,0:T(8,128)(2,1)} %all-gather.18.cloned.1.call-done, f32[768,2048]{1,0:T(8,128)} %copy-done.5, f32[2048]{0:T(1024)S(1)} %bitcast.118, f32[2048]{0:T(1024)S(1)} %bitcast.113, f32[768]{0:T(1024)S(1)} %fusion.39, ...), kind=kOutput, calls=%fused_computation.29 | convolution fusion | flops 12955680768 | bytes 54548480 | tf_op jit(solution)/shard_map/dot_general | solution.py:128
  665.9 20.8 %fusion.50 = f32[768,2048]{1,0:T(8,128)} fusion(bf16[768,4096]{1,0:T(8,128)(2,1)} %get-tuple-element.43, bf16[2048,4096]{1,0:T(8,128)(2,1)} %all-gather.18.cloned.1.call-done), kind=kOutput, calls=%fused_computation.118 | convolution fusion | flops 12884901888 | bytes 29360128 | tf_op jit(solution)/shard_map/dot_general | solution.py:28
  686.8 31.8 %convolution_convert_fusion = bf16[768,2048]{1,0:T(8,128)(2,1)} fusion(bf16[2048,4096]{1,0:T(8,128)(2,1)} %all-gather.20.cloned.1.call-done, f32[768,4096]{1,0:T(8,128)} %get-tuple-element.44), kind=kOutput, calls=%fused_computation.61 | convolution fusion | flops 12914786304 | bytes 32505856 | tf_op jit(solution)/shard_map/dot_general | solution.py:28
  718.8 119.5 %all-reduce.12.cloned.1.call-done = f32[768,2048]{1,0:T(8,128)} async-done(((f32[768,2048]{1,0:T(8,128)}), f32[768,2048]{1,0:T(8,128)}) %all-reduce.12.cloned.1.call-update) | async-done | bytes 6291472 | tf_op jit(solution)/shard_map/psum | solution.py:152
  844.9 75.4 %all-gather.22.cloned.1.call-done = bf16[1536,2048]{1,0:T(8,128)(2,1)} async-done(((bf16[768,2048]{1,0:T(8,128)(2,1)}), bf16[1536,2048]{1,0:T(8,128)(2,1)}) %all-gather.22.cloned.1.call-update) | async-done | bytes 6291472 | tf_op jit(solution)/shard_map/all_gather | solution.py:131
  954.9 12.1 fusion
  967.0 13.1 fusion.2
  986.9 22.8 %all-reduce.15 = bf16[768,256]{0,1:T(8,128)(2,1)S(1)} all-reduce(f32[768,256]{0,1:T(8,128)} %pad_maximum_fusion), channel_id=1, replica_groups=mesh['dp'=16,'tensor'=2] {'tensor'}, use_global_device_ids=true, to_apply=%region_20.21 | all-reduce | flops 196608 | bytes 1179648 | tf_op jit(solution)/shard_map/psum | solution.py:182
  1035.1 23.6 %convolution_dynamic-update-slice_fusion.1 = f32[2048,10496]{1,0:T(8,128)} fusion(f32[2048,10496]{1,0:T(8,128)} %convolution_dynamic-update-slice_fusion.2, bf16[768,4096]{1,0:T(8,128)(2,1)} %get-tuple-element.43, f32[768,2048]{1,0:T(8,128)} %copy-done.5, f32[2048]{0:T(1024)S(1)} %bitcast.119, f32[2048]{0:T(1024)S(1)} %bitcast.116, f32[768]{0:T(1024)S(1)} %fusion.39, ...), kind=kOutput, calls=%fused_computation.9 | convolution fusion | flops 12892766208 | bytes 46159872 | tf_op jit(solution)/shard_map/dot_general | solution.py:34
  1058.7 25.3 %convolution_dynamic-update-slice_fusion = f32[2048,10496]{1,0:T(8,128)} fusion(f32[2048,10496]{1,0:T(8,128)} %convolution_dynamic-update-slice_fusion.1, bf16[768,2048]{1,0:T(8,128)(2,1)} %gather_fusion.5, f32[768,4096]{1,0:T(8,128)} %get-tuple-element.44), kind=kOutput, calls=%fused_computation.8 | convolution fusion | flops 12913213440 | bytes 49283072 | tf_op jit(solution)/shard_map/dot_general | solution.py:34
  1095.4 83.1 %all-reduce.14.cloned.1.call-done = f32[768,2048]{1,0:T(8,128)} async-done(((f32[768,2048]{1,0:T(8,128)}), f32[768,2048]{1,0:T(8,128)}) %all-reduce.14.cloned.1.call-update) | async-done | bytes 6291472 | tf_op jit(solution)/shard_map/psum | solution.py:182
  1194.0 10.1 gather_fusion.6
  1220.2 100.9 %all-reduce.4 = (f32[2048]{0:T(1024)S(1)}, f32[2048]{0:T(1024)S(1)}, f32[2048]{0:T(1024)S(1)}, f32[2048]{0:T(1024)S(1)}) all-reduce(f32[2048]{0:T(1024)S(1)} %get-tuple-element.23, f32[2048]{0:T(1024)S(1)} %copy-done.36, f32[2048]{0:T(1024)S(1)} %copy-done.37, f32[2048]{0:T(1024)S(1)} %copy-done.38), channel_id=4, replica_groups=mesh['dp'=16,'tensor'=2] {'dp'}, use_global_device_ids=true, to_apply=%region_25.26.clone | all-reduce | flops 8192 | bytes 65536
  1323.4 9.6 gather_fusion.7
  1333.0 634.9 %reduce-scatter.2.cloned.1.call-done = f32[128,10496]{1,0:T(8,128)} async-done(((f32[2048,10496]{1,0:T(8,128)}), f32[128,10496]{1,0:T(8,128)}) %reduce-scatter.2.cloned.1.call-update) | async-done | bytes 5373968 | tf_op jit(solution)/shard_map/reduce_scatter | solution.py:193
  (228 shorter events, 246.4 us)
Async XLA Ops:
  7.2 173.6 %all-gather.12.cloned.1.call-start = ((), (), s32[]{:S(2)}) async-start(), calls=%async_computation.5 | async-start | bytes 1114112 | tf_op jit(solution)/shard_map/all_gather | solution.py:85
  9.0 175.2 %all-gather.14.cloned.1.call-start = ((), (), s32[]{:S(2)}) async-start(), calls=%async_computation.6 | async-start | bytes 4456448 | tf_op jit(solution)/shard_map/all_gather | solution.py:84
  20.2 128.1 %copy-start.29 = (s32[12288]{0:T(1024)S(1)}, s32[12288]{0:T(1024)}, u32[]{:S(2)}) copy-start(s32[12288]{0:T(1024)} %param.24) | copy-start | bytes 147460
  20.3 146.4 %all-to-all-start = ((bf16[16,48,2048]{2,1,0:T(8,128)(2,1)}), bf16[16,48,2048]{2,1,0:T(8,128)(2,1)S(1)}, u32[]{:S(2)}, u32[]{:S(2)}) async-start(bf16[16,48,2048]{2,1,0:T(8,128)(2,1)} %bitcast.100), calls=%async_computation | async-start | bytes 6291456 | tf_op jit(solution)/shard_map/all_to_all | solution.py:78
  27.8 192.0 %all-gather.16.cloned.1.call-start = ((), (), s32[]{:S(2)}) async-start(), calls=%async_computation.7 | async-start | bytes 4456448 | tf_op jit(solution)/shard_map/all_gather | solution.py:86
  29.7 349.1 %all-reduce.10.cloned.1.call-start = ((), (), s32[]{:S(2)}) async-start(), calls=%async_computation.8 | async-start | bytes 12582912 | tf_op jit(solution)/shard_map/psum | solution.py:125
  228.1 279.7 %all-gather.20.cloned.1.call-start = ((), (), s32[]{:S(2)}) async-start(), calls=%async_computation.10 | async-start | bytes 17825792 | tf_op jit(solution)/shard_map/all_gather | solution.py:88
  231.0 404.0 %all-gather.18.cloned.1.call-start = ((), (), s32[]{:S(2)}) async-start(), calls=%async_computation.9 | async-start | bytes 17825792 | tf_op jit(solution)/shard_map/all_gather | solution.py:87
  238.4 71.0 %copy-start.51 = (f32[128]{0:T(128)S(1)}, f32[128]{0:T(128)}, u32[]{:S(2)}) copy-start(f32[128]{0:T(128)} %param.22) | copy-start | bytes 1540
  238.4 103.8 %all-to-all-start.2 = ((bf16[16,48,2048]{2,1,0:T(8,128)(2,1)}), bf16[16,48,2048]{2,1,0:T(8,128)(2,1)S(1)}, u32[]{:S(2)}, u32[]{:S(2)}) async-start(bf16[16,48,2048]{2,1,0:T(8,128)(2,1)} %bitcast.103), calls=%async_computation.2 | async-start | bytes 6291456 | tf_op jit(solution)/shard_map/all_to_all | solution.py:79
  242.3 596.0 %all-reduce.12.cloned.1.call-start = ((), (), s32[]{:S(2)}) async-start(), calls=%async_computation.11 | async-start | bytes 12582912 | tf_op jit(solution)/shard_map/psum | solution.py:152
  309.4 325.7 %copy-start.43 = (f32[16,1,128]{2,1,0:T(1,128)}, f32[16,1,128]{2,1,0:T(1,128)S(1)}, u32[]{:S(2)}) copy-start(f32[16,1,128]{2,1,0:T(1,128)S(1)} %convert_element_type.162) | copy-start | bytes 24580
  383.2 124.7 %copy-start.7 = (bf16[768,2048]{1,0:T(8,128)(2,1)S(1)}, bf16[768,2048]{1,0:T(8,128)(2,1)}, u32[]{:S(2)}) copy-start(bf16[768,2048]{1,0:T(8,128)(2,1)} %gather_fusion.5) | copy-start | bytes 9437188
  686.7 233.5 %all-gather.22.cloned.1.call-start = ((), (), s32[]{:S(2)}) async-start(), calls=%async_computation.14 | async-start | bytes 9437184 | tf_op jit(solution)/shard_map/all_gather | solution.py:131
  686.8 31.9 %copy-start.20 = (f32[8,768]{1,0:T(8,128)S(1)}, f32[8,768]{1,0:T(8,128)}, u32[]{:S(2)}) copy-start(f32[8,768]{1,0:T(8,128)} %copy-done.19) | copy-start | bytes 73732
  686.8 31.9 %copy-start.26 = (f32[8,768]{1,0:T(8,128)S(1)}, f32[8,768]{1,0:T(8,128)}, u32[]{:S(2)}) copy-start(f32[8,768]{1,0:T(8,128)} %copy-done.25) | copy-start | bytes 73732
  718.7 459.8 %all-reduce.14.cloned.1.call-start = ((), (), s32[]{:S(2)}) async-start(), calls=%async_computation.12 | async-start | bytes 12582912 | tf_op jit(solution)/shard_map/psum | solution.py:182
  1024.4 943.6 %reduce-scatter.2.cloned.1.call-start = ((), (), s32[]{:S(2)}) async-start(), calls=%async_computation.13 | async-start | bytes 91357184 | tf_op jit(solution)/shard_map/reduce_scatter | solution.py:193
  1089.6 88.9 %copy-start.22 = (f32[16,1,128]{2,1,0:T(1,128)S(1)}, f32[16,1,128]{2,1,0:T(1,128)}, u32[]{:S(2)}) copy-start(f32[16,1,128]{2,1,0:T(1,128)} %copy-done.21) | copy-start | bytes 24580
  1089.6 88.9 %copy-start.24 = (f32[768]{0:T(1024)S(1)}, f32[768]{0:T(1024)}, u32[]{:S(2)}) copy-start(f32[768]{0:T(1024)} %copy-done.23) | copy-start | bytes 9220
  1089.6 114.5 %all-to-all-start.1 = ((bf16[16,48,2048]{2,1,0:T(8,128)(2,1)}), bf16[16,48,2048]{2,1,0:T(8,128)(2,1)S(1)}, u32[]{:S(2)}, u32[]{:S(2)}) async-start(bf16[16,48,2048]{2,1,0:T(8,128)(2,1)} %bitcast.102), calls=%async_computation.1 | async-start | bytes 6291456 | tf_op jit(solution)/shard_map/all_to_all | solution.py:222
  1095.4 89.3 %copy-start.28 = (f32[768]{0:T(1024)S(1)}, f32[768]{0:T(1024)}, u32[]{:S(2)}) copy-start(f32[768]{0:T(1024)} %copy-done.27) | copy-start | bytes 9220
  1204.1 119.4 %all-to-all-start.3 = ((bf16[16,48,2048]{2,1,0:T(8,128)(2,1)}), bf16[16,48,2048]{2,1,0:T(8,128)(2,1)}, u32[]{:S(2)}, u32[]{:S(2)}) async-start(bf16[16,48,2048]{2,1,0:T(8,128)(2,1)} %bitcast.101), calls=%async_computation.3 | async-start | bytes 6291456 | tf_op jit(solution)/shard_map/all_to_all | solution.py:223
  1323.4 653.0 %copy-start.1 = (bf16[768,2048]{1,0:T(8,128)(2,1)S(1)}, bf16[768,2048]{1,0:T(8,128)(2,1)}, u32[]{:S(2)}) copy-start(bf16[768,2048]{1,0:T(8,128)(2,1)} %param.13) | copy-start | bytes 9437188
  (45 other events, 310.9 us)
Sparse Core Ops, SparseCore 0:
  10.7 62.2 all-gather.11
  75.7 56.6 all-gather.13
  134.6 50.0 all-gather.15
  228.2 150.4 all-reduce.9
  381.3 126.4 all-gather.19
  510.4 124.5 all-gather.17
  686.9 151.4 all-reduce.11
  839.9 80.3 all-gather.21
  1024.5 153.9 all-reduce.13
  1182.6 785.3 reduce-scatter.1
